TPU v7x, 256 devices: a whole 4x4x8 slice. The times are simulated.
256 devices in a mesh: pq: 8 (over z_hi, x), rs: 32 (over y, z_lo, core).
Axes of the slice: x: 4, y: 4, z: 8 (z_hi: 2, z_lo: 4; z = z_hi * 4 + z_lo), core: 2. Of those that a mesh axis runs over, the one named last changes fastest.
Arguments:
- integrals: bfloat16 [512, 1152, 1152], P('pq', 'rs'), may hold values from -6 to 6
- coeff: bfloat16 [1152, 896], P('rs', 'pq'), may hold values from -0.1875 to 0.1875
Outputs:
- half_mo: bfloat16 [512, 896, 896], P('pq', 'rs')
All inputs are finite; a program needn't handle non-finite values.
Results may differ from a plain program's by a relative error of at most 0.0049.
Values may be sent and summed in bfloat16 or wider, within the bound.
No kernel may reach another device: no remote copies, remote signals or barrier semaphores. Data moves between devices by JAX's collectives and lax.ppermute only.
A program may use at most 128 MiB of HBM per device.

v0:
```python
import jax
import jax.numpy as jnp
from jax import lax
from jax.sharding import PartitionSpec as P

NBASIS = 1152
NORB = 896


def joined_along(parts, dim):
    parts = jnp.moveaxis(parts, 0, dim)
    lengths = parts.shape
    return parts.reshape(*lengths[:dim], lengths[dim] * lengths[dim + 1], *lengths[dim + 2 :])


def from_everyone(array, axis):
    count = lax.axis_size(axis)
    return lax.all_to_all(
        jnp.broadcast_to(array[None], (count, *array.shape)), axis, 0, 0, tiled=True
    )


def collect(array, axis, dim):
    return joined_along(from_everyone(array, axis), dim)


def second_half(received, panel):
    return jnp.einsum("prl,rk->plk", received, panel, preferred_element_type=jnp.float32).astype(
        jnp.bfloat16
    )


def on_device(integrals, coeff):
    pair_rows = integrals.shape[0]
    block_rows = integrals.shape[1]
    flat = integrals.reshape(pair_rows * block_rows, NBASIS)
    strip = collect(coeff, "pq", 1)
    panel = collect(strip, "rs", 0)
    first = jnp.dot(flat, panel, preferred_element_type=jnp.float32).astype(jnp.bfloat16)
    first = first.reshape(pair_rows, block_rows, NORB)
    return second_half(lax.all_to_all(first, "rs", split_axis=2, concat_axis=1, tiled=True), panel)


def solution(mesh):
    placed = (P("pq", "rs", None), P("rs", "pq"))
    return jax.shard_map(
        on_device, mesh=mesh, in_specs=placed, out_specs=P("pq", "rs", None), check_vma=False
    )
```

profile of v0, /device:TPU:1, one launch (start us, length us, event | category | flops | bytes accessed | tf_op | source)
XLA Modules:
  0.0 255.1 jit_solution(5755505084666371884)
XLA Ops:
  0.0 0.7 broadcast_in_dim.6
  0.7 20.4 %all_to_all.25 = bf16[8,36,112]{2,1,0:T(8,128)(2,1)S(1)} all-to-all(bf16[8,36,112]{2,1,0:T(8,128)(2,1)S(1)} %broadcast_in_dim.6), channel_id=1, replica_groups=mesh['pq'=8,'rs'=32] {'pq'}, dimensions={0} | all-to-all | bytes 129024 | tf_op jit(solution)/shard_map/all_to_all | solution.py:18
  21.1 0.1 broadcast_in_dim.14
  21.3 1.6 broadcast_in_dim.15
  22.8 8.1 %all-to-all-start.1 = ((bf16[32,36,896]{2,1,0:T(8,128)(2,1)}), bf16[32,36,896]{2,1,0:T(8,128)(2,1)S(1)}, u32[]{:S(2)}, u32[]{:S(2)}) async-start(bf16[32,36,896]{2,1,0:T(8,128)(2,1)} %broadcast_in_dim.15), calls=%async_computation.1 | async-start | bytes 4587520 | tf_op jit(solution)/shard_map/all_to_all | solution.py:18
  30.9 8.0 %copy.15 = bf16[64,36,1152]{2,1,0:T(8,128)(2,1)} copy(bf16[64,36,1152]{2,0,1:T(8,128)(2,1)} %param.2) | data formatting | bytes 10616832 | tf_op args[0]
  39.0 8.9 %reshape.11 = bf16[2304,1152]{1,0:T(8,128)(2,1)} reshape(bf16[64,36,1152]{2,1,0:T(8,128)(2,1)} %copy.15) | data formatting | bytes 10616832 | tf_op jit(solution)/shard_map/reshape | solution.py:36
  47.8 37.1 %all-to-all-done.1 = bf16[32,36,896]{2,1,0:T(8,128)(2,1)S(1)} async-done(((bf16[32,36,896]{2,1,0:T(8,128)(2,1)}), bf16[32,36,896]{2,1,0:T(8,128)(2,1)S(1)}, u32[]{:S(2)}, u32[]{:S(2)}) %all-to-all-start.1) | async-done | bytes 2064416 | tf_op jit(solution)/shard_map/all_to_all | solution.py:18
  84.9 1.9 reshape.12
  86.9 10.0 %convolution_convert_fusion = bf16[2304,896]{1,0:T(8,128)(2,1)} fusion(bf16[2304,1152]{1,0:T(8,128)(2,1)} %reshape.11, bf16[1152,896]{1,0:T(8,128)(2,1)} %reshape.12), kind=kOutput, calls=%fused_computation.4 | convolution fusion | flops 4758405120 | bytes 11501568 | tf_op jit(solution)/shard_map/dot_general | solution.py:39
  96.8 6.9 %reshape.13 = bf16[64,36,896]{2,1,0:T(8,128)(2,1)} reshape(bf16[2304,896]{1,0:T(8,128)(2,1)} %convolution_convert_fusion) | data formatting | bytes 8257536 | tf_op jit(solution)/shard_map/reshape | solution.py:40
  103.7 13.9 %copy.17 = bf16[64,36,896]{0,1,2:T(8,128)(2,1)} copy(bf16[64,36,896]{2,1,0:T(8,128)(2,1)} %reshape.13) | data formatting | bytes 8257536 | tf_op jit(solution)/shard_map/reshape | solution.py:40
  117.6 13.7 %reshape.16 = bf16[32,2,32256]{2,1,0:T(2,128)(2,1)} reshape(bf16[896,36,64]{2,1,0:T(8,128)(2,1)} %bitcast.18) | data formatting | bytes 8257536
  131.3 99.3 %all_to_all.26 = bf16[32,2,32256]{2,1,0:T(2,128)(2,1)} all-to-all(bf16[32,2,32256]{2,1,0:T(2,128)(2,1)} %reshape.16), channel_id=1, replica_groups=mesh['pq'=8,'rs'=32] {'rs'}, dimensions={0} | all-to-all | bytes 8257536 | tf_op jit(solution)/shard_map/all_to_all | solution.py:41
  230.6 14.6 %reshape.17 = bf16[896,36,64]{2,1,0:T(8,128)(2,1)} reshape(bf16[32,2,32256]{2,1,0:T(2,128)(2,1)} %all_to_all.26) | data formatting | bytes 8257536
  245.2 9.9 %bitcast_convert_fusion = bf16[64,28,896]{2,0,1:T(8,128)(2,1)} fusion(bf16[64,36,32,28]{0,1,3,2:T(8,128)(2,1)} %bitcast.17, bf16[32,36,896]{2,1,0:T(8,128)(2,1)S(1)} %all-to-all-done.1), kind=kOutput, calls=%fused_computation.3 | convolution fusion | flops 3700981760 | bytes 9404416 | tf_op jit(solution)/shard_map/prl,rk->plk/dot_general | solution.py:28
  (1 shorter events, 0.0 us)
Async XLA Ops:
  22.8 62.1 %all-to-all-start.1 = ((bf16[32,36,896]{2,1,0:T(8,128)(2,1)}), bf16[32,36,896]{2,1,0:T(8,128)(2,1)S(1)}, u32[]{:S(2)}, u32[]{:S(2)}) async-start(bf16[32,36,896]{2,1,0:T(8,128)(2,1)} %broadcast_in_dim.15), calls=%async_computation.1 | async-start | bytes 4587520 | tf_op jit(solution)/shard_map/all_to_all | solution.py:18
where the time goes:
time: 257 us; the launch traced here: 255 us
  blocking collectives  120 us (47%)
  local copies, waits for them, and re-layouts  70.4 us (27%)
  waiting for transfers between devices  37.1 us (14%)
  matrix products  19.8 us (8%)
  starting transfers between devices  8.09 us (3%)
    all_to_all x1, blocking collectives, on_device(): lax.all_to_all(first, 'rs', split_axis=2, concat_axis=1, tiled=True)  99.3 us
    all_to_all x1, waiting for transfers between devices, from_everyone(): lax.all_to_all(jnp.broadcast_to(array[None], (count, *array.shape)), axis...  37.1 us
    unnamed x3, local copies, waits for them, and re-layouts  36.4 us
    reshape x2, local copies, waits for them, and re-layouts, on_device(): first = first.reshape(pair_rows, block_rows, NORB)  20.8 us
    all_to_all x1, blocking collectives, from_everyone(): lax.all_to_all(jnp.broadcast_to(array[None], (count, *array.shape)), axis...  20.4 us
    dot_general x1, matrix products, on_device(): jnp.dot(flat, panel, preferred_element_type=jnp.float32)  9.95 us
    dot_general x1, matrix products, second_half(): jnp.einsum('prl,rk->plk', received, panel, preferred_element_type=jnp.flo...  9.88 us
    reshape x1, local copies, waits for them, and re-layouts, on_device(): flat = integrals.reshape(pair_rows * block_rows, NBASIS)  8.88 us
  transfers between devices with their start and end apart: 1, of which 1 were waited for; matrix products, arithmetic and copies ran while one was open for 7% of the time, Pallas kernels for 0%

commit v1 on v0

--- a/solution.py
+++ b/solution.py
@@ -38,7 +38,13 @@
     panel = collect(strip, "rs", 0)
     first = jnp.dot(flat, panel, preferred_element_type=jnp.float32).astype(jnp.bfloat16)
     first = first.reshape(pair_rows, block_rows, NORB)
-    return second_half(lax.all_to_all(first, "rs", split_axis=2, concat_axis=1, tiled=True), panel)
+    return second_half(
+        jnp.concatenate(
+            lax.all_to_all(jnp.stack(jnp.split(first, lax.axis_size("rs"), 2), axis=0), "rs", 0, 0),
+            1,
+        ),
+        panel,
+    )
 
 
 def solution(mesh):

time: 257 us -> 320 us (1.25)
  local copies, waits for them, and re-layouts: 70.4 us -> 133 us
    unnamed x3 -> x38, local copies, waits for them, and re-layouts: 36.4 us -> 88.4 us
    another operation x0 -> x2, local copies, waits for them, and re-layouts: none -> 24.5 us  [on_device(): jnp.stack(jnp.split(first, lax.axis_size('rs'), 2), axis=0)]
    reshape x2 -> x1, local copies, waits for them, and re-layouts: 20.8 us -> 6.94 us  [on_device(): first = first.reshape(pair_rows, block_rows, NORB)]
  transfers between devices with their start and end apart: 1 -> 1, of which waited for: 1 -> 1; matrix products, arithmetic and copies ran while one was open for 7% -> 5% of each run, Pallas kernels for 0% -> 0%
where the time goes in v1:
time: 320 us; the launch traced here: 318 us
  local copies, waits for them, and re-layouts  133 us (42%)
  blocking collectives  120 us (38%)
  waiting for transfers between devices  37 us (12%)
  matrix products  19.9 us (6%)
  starting transfers between devices  8.09 us (3%)
    all_to_all x1, blocking collectives, on_device(): lax.all_to_all(jnp.stack(jnp.split(first, lax.axis_size('rs'), 2), axis=0...  99.3 us
    unnamed x38, local copies, waits for them, and re-layouts  88.4 us
    all_to_all x1, waiting for transfers between devices, from_everyone(): lax.all_to_all(jnp.broadcast_to(array[None], (count, *array.shape)), axis...  37 us
    another operation x2, local copies, waits for them, and re-layouts, on_device(): jnp.stack(jnp.split(first, lax.axis_size('rs'), 2), axis=0)  24.5 us
    all_to_all x1, blocking collectives, from_everyone(): lax.all_to_all(jnp.broadcast_to(array[None], (count, *array.shape)), axis...  20.4 us
    dot_general x1, matrix products, on_device(): jnp.dot(flat, panel, preferred_element_type=jnp.float32)  9.96 us
    dot_general x1, matrix products, second_half(): jnp.einsum('prl,rk->plk', received, panel, preferred_element_type=jnp.flo...  9.96 us
    reshape x1, local copies, waits for them, and re-layouts, on_device(): flat = integrals.reshape(pair_rows * block_rows, NBASIS)  8.91 us
  transfers between devices with their start and end apart: 1, of which 1 were waited for; matrix products, arithmetic and copies ran while one was open for 5% of the time, Pallas kernels for 0%

profile of v1, /device:TPU:1, one launch (start us, length us, event | category | flops | bytes accessed | tf_op | source)
XLA Modules:
  0.0 318.0 jit_solution(9949122319314009600)
XLA Ops:
  0.0 0.7 broadcast_in_dim.6
  0.7 20.4 %all_to_all.15 = bf16[8,36,112]{2,1,0:T(8,128)(2,1)S(1)} all-to-all(bf16[8,36,112]{2,1,0:T(8,128)(2,1)S(1)} %broadcast_in_dim.6), channel_id=1, replica_groups=mesh['pq'=8,'rs'=32] {'pq'}, dimensions={0} | all-to-all | bytes 129024 | tf_op jit(solution)/shard_map/all_to_all | solution.py:18
  21.1 0.1 broadcast_in_dim.14
  21.3 1.6 broadcast_in_dim.15
  22.8 8.1 %all-to-all-start.1 = ((bf16[32,36,896]{2,1,0:T(8,128)(2,1)}), bf16[32,36,896]{2,1,0:T(8,128)(2,1)S(1)}, u32[]{:S(2)}, u32[]{:S(2)}) async-start(bf16[32,36,896]{2,1,0:T(8,128)(2,1)} %broadcast_in_dim.15), calls=%async_computation.1 | async-start | bytes 4587520 | tf_op jit(solution)/shard_map/all_to_all | solution.py:18
  30.9 8.0 %copy.109 = bf16[64,36,1152]{2,1,0:T(8,128)(2,1)} copy(bf16[64,36,1152]{2,0,1:T(8,128)(2,1)} %param.2) | data formatting | bytes 10616832 | tf_op args[0]
  39.0 8.9 %reshape.15 = bf16[2304,1152]{1,0:T(8,128)(2,1)} reshape(bf16[64,36,1152]{2,1,0:T(8,128)(2,1)} %copy.109) | data formatting | bytes 10616832 | tf_op jit(solution)/shard_map/reshape | solution.py:36
  47.9 37.0 %all-to-all-done.1 = bf16[32,36,896]{2,1,0:T(8,128)(2,1)S(1)} async-done(((bf16[32,36,896]{2,1,0:T(8,128)(2,1)}), bf16[32,36,896]{2,1,0:T(8,128)(2,1)S(1)}, u32[]{:S(2)}, u32[]{:S(2)}) %all-to-all-start.1) | async-done | bytes 2064416 | tf_op jit(solution)/shard_map/all_to_all | solution.py:18
  84.9 1.9 reshape.16
  86.9 10.0 %convolution_convert_fusion = bf16[2304,896]{1,0:T(8,128)(2,1)} fusion(bf16[2304,1152]{1,0:T(8,128)(2,1)} %reshape.15, bf16[1152,896]{1,0:T(8,128)(2,1)} %reshape.16), kind=kOutput, calls=%fused_computation.3 | convolution fusion | flops 4758405120 | bytes 11501568 | tf_op jit(solution)/shard_map/dot_general | solution.py:39
  96.8 6.9 %reshape.17 = bf16[64,36,896]{2,1,0:T(8,128)(2,1)} reshape(bf16[2304,896]{1,0:T(8,128)(2,1)} %convolution_convert_fusion) | data formatting | bytes 8257536 | tf_op jit(solution)/shard_map/reshape | solution.py:40
  103.8 0.0 slice-start
  103.8 2.1 fusion.36
  105.9 2.2 fusion.35
  108.1 2.2 fusion.34
  110.3 2.2 fusion.33
  112.4 2.4 fusion.32
  114.8 2.2 fusion.31
  117.0 2.2 fusion.30
  119.2 2.2 fusion.29
  121.3 0.0 slice-start.1
  121.3 2.3 fusion.28
  123.6 2.4 fusion.27
  126.0 2.2 fusion.26
  128.2 2.1 fusion.25
  130.4 2.2 fusion.24
  132.6 2.5 fusion.23
  135.1 2.2 fusion.22
  137.2 2.1 fusion.21
  139.4 0.0 slice-done
  139.4 0.0 slice-done.1
  139.4 1.1 fusion.20
  140.5 1.1 fusion.19
  141.5 1.1 fusion.18
  142.6 1.1 fusion.17
  143.8 1.1 fusion.16
  144.9 1.1 fusion.15
  146.0 1.1 fusion.14
  147.1 1.1 fusion.13
  148.2 1.1 fusion.12
  149.3 1.1 fusion.11
  150.4 1.1 fusion.10
  151.5 1.1 fusion.9
  152.6 1.1 fusion.8
  153.7 1.1 fusion.7
  154.8 1.1 fusion.6
  155.9 1.1 fusion.5
  156.9 23.5 %copy.111 = bf16[32,64,36,28]{1,2,3,0:T(8,128)(2,1)} copy(bf16[32,64,36,28]{3,2,1,0:T(8,128)(2,1)} %fusion.5) | data formatting | bytes 8257536 | tf_op jit(solution)/shard_map/stack | solution.py:43
  180.4 13.7 %reshape.21 = bf16[32,2,32256]{2,1,0:T(2,128)(2,1)} reshape(bf16[32,28,36,64]{3,2,1,0:T(8,128)(2,1)} %bitcast.151) | data formatting | bytes 8257536
  194.1 99.3 %all_to_all.16 = bf16[32,2,32256]{2,1,0:T(2,128)(2,1)} all-to-all(bf16[32,2,32256]{2,1,0:T(2,128)(2,1)} %reshape.21), channel_id=1, replica_groups=mesh['pq'=8,'rs'=32] {'rs'}, dimensions={0} | all-to-all | bytes 8257536 | tf_op jit(solution)/shard_map/all_to_all | solution.py:43
  293.4 14.6 %reshape.22 = bf16[32,28,36,64]{3,2,1,0:T(8,128)(2,1)} reshape(bf16[32,2,32256]{2,1,0:T(2,128)(2,1)} %all_to_all.16) | data formatting | bytes 8257536
  308.0 10.0 %bitcast_convert_fusion = bf16[64,28,896]{2,0,1:T(8,128)(2,1)} fusion(bf16[32,36,896]{2,1,0:T(8,128)(2,1)S(1)} %all-to-all-done.1, bf16[32,28,36,64]{3,2,1,0:T(8,128)(2,1)} %reshape.22), kind=kOutput, calls=%fused_computation.2 | convolution fusion | flops 3700981760 | bytes 9404416 | tf_op jit(solution)/shard_map/prl,rk->plk/dot_general | solution.py:28
  (2 shorter events, 0.0 us)
Async XLA Ops:
  22.8 62.1 %all-to-all-start.1 = ((bf16[32,36,896]{2,1,0:T(8,128)(2,1)}), bf16[32,36,896]{2,1,0:T(8,128)(2,1)S(1)}, u32[]{:S(2)}, u32[]{:S(2)}) async-start(bf16[32,36,896]{2,1,0:T(8,128)(2,1)} %broadcast_in_dim.15), calls=%async_computation.1 | async-start | bytes 4587520 | tf_op jit(solution)/shard_map/all_to_all | solution.py:18
  103.8 35.6 %slice-start = ((s8[4587520]{0:T(1024)(128)(4,1)}), s8[4194304]{0:T(1024)(128)(4,1)S(1)}, s32[]{:S(2)}) async-start(s8[4587520]{0:T(1024)(128)(4,1)} %bitcast.149), calls=%async_computation.3 | async-start | bytes 8388608
  121.3 18.0 %slice-start.1 = ((s8[4587520]{0:T(1024)(128)(4,1)}), s8[393216]{0:T(1024)(128)(4,1)S(1)}, s32[]{:S(2)}) async-start(s8[4587520]{0:T(1024)(128)(4,1)} %bitcast.149), calls=%async_computation.4 | async-start | bytes 786432
